TPU v7x, 32 devices: a whole 2x2x4 slice. The times are simulated.
32 devices in a mesh: tm: 4 (over y, x), space: 8 (over z, core).
Axes of the slice: x: 2, y: 2, z: 4, core: 2. Of those that a mesh axis runs over, the one named last changes fastest.
Arguments:
- states: float32 [4, 256, 256, 256], P('tm', 'space'), may hold values from -4 to 4
- forcing: float32 [4, 256, 256, 256], P('tm', 'space'), may hold values from -4 to 4
- inflow: float32 [256, 256, 256], P('space'), may hold values from -4 to 4
- timestep: float32 [1], replicated, may hold values from 0.05 to 0.2
Outputs:
- new_states: float32 [4, 256, 256, 256], P('tm', 'space')
- defects: float32 [4, 256, 256, 256], P('tm', 'space')
All inputs are finite; a program needn't handle non-finite values.
Results may differ from a plain program's by a relative error of at most 0.00013.
Values sent between devices are 32-bit elements; how exact they have to be, the bound alone decides.
A program may use at most 192 MiB of HBM per device.

v0:
```python
import math

import jax
import jax.numpy as jnp
from jax import lax
from jax.sharding import PartitionSpec as P

FINE = 8


highest = lax.Precision.HIGHEST


def shifted(array, axis, by):
    length = lax.axis_size(axis)
    pairs = [(i, i + by) for i in range(length) if 0 <= i + by < length]
    return lax.ppermute(array, axis, pairs)


def prefix(part, axis, combine, identity):
    place = lax.axis_index(axis)
    gathered = jax.tree.map(lambda a: lax.all_gather(a, axis), part)
    state = jax.tree.map(lambda a, e: jnp.zeros_like(a) + jnp.asarray(e, a.dtype), part, identity)

    def one(lap, state):
        return combine(
            state, jax.tree.map(lambda a: lax.dynamic_index_in_dim(a, lap, 0, False), gathered)
        )

    return lax.fori_loop(0, place, one, state)


def hartley_table(extent):
    wavenumber = jnp.arange(extent, dtype=jnp.int32)
    product = wavenumber[:, None] * wavenumber[None, :] % extent
    angles = product.astype(jnp.float32) * (2.0 * math.pi / extent)
    return (jnp.cos(angles) + jnp.sin(angles)) * (1.0 / math.sqrt(extent))


def lattice_symbol(wavenumber, extent):
    angles = (wavenumber % extent).astype(jnp.float32) * (2.0 * math.pi / extent)
    return 2.0 - 2.0 * jnp.cos(angles)


def planar_forward(fields, hartley):
    rows_done = jnp.einsum("pzxy,ky->pzxk", fields, hartley, precision=highest)
    return jnp.einsum("pzxy,kx->pzky", rows_done, hartley, precision=highest)


def on_device(states, forcing, inflow, timestep):
    planes = states.shape[1]
    extent = states.shape[2]
    hartley = hartley_table(extent)
    stepsize = timestep[0]

    def depth_inverse(spectrum):
        return jnp.einsum("pkxy,kz->pzxy", spectrum, hartley, precision=highest)

    def width_inverse(blocks):
        return jnp.einsum("pzky,kx->pzxy", blocks, hartley, precision=highest)

    def planar_tail(blocks):
        return jnp.einsum("pzxk,ky->pzxy", blocks, hartley, precision=highest)

    stacked = jnp.concatenate([states, forcing, inflow[None]], axis=0)
    spectra = jnp.einsum(
        "pzxy,kz->pkxy",
        lax.all_to_all(
            planar_forward(stacked, hartley), "space", split_axis=2, concat_axis=1, tiled=True
        ),
        hartley,
        precision=highest,
    )
    spec_states = spectra[0:1]
    spec_forcing = spectra[1:2]
    spec_inflow = spectra[2:3]
    column = lax.axis_index("space") * planes + jnp.arange(planes, dtype=jnp.int32)
    full_symbol = lattice_symbol(jnp.arange(extent, dtype=jnp.int32), extent)
    local_symbol = lattice_symbol(column, extent)
    laplace = (
        lattice_symbol(jnp.arange(extent, dtype=jnp.int32), extent)[:, None, None]
        + local_symbol[None, :, None]
        + full_symbol[None, None, :]
    )
    damping = 1.0 / (1.0 + stepsize * laplace)
    propagator = jnp.ones_like(damping)
    accrued = jnp.zeros_like(damping)
    for repeat in range(FINE):
        propagator = propagator * damping
        accrued = accrued + propagator
    coarse = 1.0 / (1.0 + FINE * stepsize * laplace)
    propagator, source_gain, coarse = (propagator, stepsize * accrued, coarse)
    coarse_log = jnp.log(coarse)
    advanced = propagator * spec_states + source_gain * spec_forcing
    arrived = shifted(advanced, "tm", 1)
    opening = lax.axis_index("tm") == 0
    relaxed = jnp.where(opening, spec_inflow, arrived)
    defect_spec = propagator * (relaxed - spec_states)

    def compose(former, latter):
        return (former[0] + latter[0], jnp.exp(latter[0] * coarse_log) * former[1] + latter[1])

    single = jnp.ones((), jnp.float32)
    empty = (jnp.zeros((), jnp.float32), jnp.zeros_like(defect_spec))
    counted, correction = prefix((single, defect_spec), "tm", compose, empty)
    updated = relaxed + correction
    defect_field = width_inverse(
        lax.all_to_all(depth_inverse(defect_spec), "space", split_axis=1, concat_axis=2, tiled=True)
    )
    defect_out = planar_tail(defect_field)
    state_field = width_inverse(
        lax.all_to_all(depth_inverse(updated), "space", split_axis=1, concat_axis=2, tiled=True)
    )
    return (planar_tail(state_field), defect_out)


def solution(mesh):
    return jax.shard_map(
        on_device,
        mesh=mesh,
        in_specs=(
            P("tm", "space", None, None),
            P("tm", "space", None, None),
            P("space", None, None),
            P(),
        ),
        out_specs=(P("tm", "space", None, None), P("tm", "space", None, None)),
        check_vma=False,
    )
```

profile of v0, /device:TPU:6, one launch (start us, length us, event | category | flops | bytes accessed | tf_op | source)
XLA Modules:
  0.0 1498.1 jit_solution(14921202936366885212)
XLA Ops:
  7.2 1.1 fusion.127
  8.2 26.0 %fusion.3 = f32[3,32,256,256]{3,2,1,0:T(8,128)} fusion(f32[1,32,256,256]{3,2,1,0:T(8,128)} %bitcast.113, f32[1,32,256,256]{3,2,1,0:T(8,128)} %param.7, f32[1,32,256,256]{3,2,1,0:T(8,128)} %param.6, f32[256,256,1,1]{1,0,3,2:T(8,128)S(1)} %fusion.127), kind=kOutput, calls=%fused_computation.5 | convolution fusion | flops 19339935744 | bytes 50593792 | tf_op jit(solution)/shard_map/pzxy,ky->pzxk/dot_general | solution.py:46
  34.3 33.0 %convolution_bitcast_fusion.1 = f32[3,32,256,256]{3,2,1,0:T(8,128)} fusion(f32[3,32,256,256]{3,2,1,0:T(8,128)} %fusion.3), kind=kOutput, calls=%fused_computation.22 | convolution fusion | flops 19328401408 | bytes 50331648 | tf_op jit(solution)/shard_map/pzxy,kx->pzky/dot_general | solution.py:47
  67.3 25.1 %copy.16 = f32[3,32,256,256]{3,1,0,2:T(8,128)} copy(f32[3,32,256,256]{3,2,1,0:T(8,128)} %convolution_bitcast_fusion.1) | data formatting | bytes 50331648 | tf_op jit(solution)/shard_map/pzxy,kx->pzky/transpose | solution.py:47
  92.4 6.4 all-to-all-start
  98.8 0.0 all-gather.3.cloned.1.call-start
  99.5 0.1 fusion.69
  99.6 0.1 broadcast_add_fusion
  99.7 0.1 copy.18
  99.8 542.4 %all-to-all-done = f32[3,32,256,256]{3,1,0,2:T(8,128)} async-done(((f32[3,32,256,256]{3,1,0,2:T(8,128)}), f32[3,32,256,256]{3,1,0,2:T(8,128)}, u32[]{:S(2)}, u32[]{:S(2)}) %all-to-all-start) | async-done | bytes 25165856 | tf_op jit(solution)/shard_map/all_to_all | solution.py:68
  642.2 17.8 %copy.17 = f32[3,32,8,32,256]{4,1,2,3,0:T(8,128)} copy(f32[3,32,8,32,256]{4,1,0,3,2:T(8,128)} %bitcast.7) | data formatting | bytes 50331648 | tf_op jit(solution)/shard_map/all_to_all | solution.py:68
  660.0 32.5 %convolution_bitcast_fusion = f32[3,256,32,256]{3,1,2,0:T(8,128)} fusion(f32[3,256,32,256]{3,1,2,0:T(8,128)} %bitcast.109), kind=kOutput, calls=%fused_computation.21 | convolution fusion | flops 19328401408 | bytes 50331648 | tf_op jit(solution)/shard_map/pzxy,kz->pkxy/dot_general | solution.py:66
  692.5 12.0 fusion.22
  704.5 1.3 collective-permute-start
  705.8 182.8 %collective-permute-done = f32[1,256,32,256]{3,1,2,0:T(8,128)} collective-permute-done((f32[1,256,32,256]{3,1,2,0:T(8,128)}, f32[1,256,32,256]{3,1,2,0:T(8,128)}, u32[]{:S(2)}, u32[]{:S(2)}) %collective-permute-start) | collective-permute-done | bytes 8388640 | tf_op jit(solution)/shard_map/ppermute | solution.py:17
  888.6 10.0 subtract_multiply_fusion
  898.6 0.0 copy-start
  898.6 3.4 copy-done
  902.0 8.3 copy.19
  910.3 0.0 all-gather.3.cloned.1.call-update
  910.3 13.1 fusion.34
  923.4 10.1 copy.27
  933.6 0.0 copy-start.1
  933.6 5.1 all-to-all-start.2
  938.7 0.0 copy-done.1
  938.7 0.6 dynamic-slice
  939.3 0.8 dynamic-update-slice
  940.0 8.9 all-reduce
  948.9 257.1 %all-gather.3.cloned.1.call-done = f32[4,256,32,256]{3,2,1,0:T(8,128)} async-done(((f32[1,256,32,256]{3,2,1,0:T(8,128)}), f32[4,256,32,256]{3,2,1,0:T(8,128)}) %all-gather.3.cloned.1.call-update) | async-done | bytes 33554448 | tf_op jit(solution)/shard_map/all_gather | solution.py:22
  1206.1 4.5 broadcast_in_dim.6
  1210.5 37.8 %while.13 = (s32[]{:T(128)}, f32[1,256,32,256]{3,2,1,0:T(8,128)}, s32[]{:T(128)}, f32[4]{0:T(128)S(1)}, f32[4,1,256,32,256]{4,3,2,1,0:T(8,128)}, /*index=5*/f32[...) while((s32[]{:T(128)}, f32[1,256,32,256]{3,2,1,0:T(8,128)}, ...), condition=%wide.region_1.2_spmd.clone, body=%wide.region_0.1_spmd.clone.sunk | while | flops 14680069 | bytes 25199792 | solution.py:30
  1210.5 0.6 dynamic_slice.16
  1211.1 12.0 bitcast_add_fusion.2
  1223.1 0.6 dynamic_slice.16
  1223.7 12.0 bitcast_add_fusion.2
  1235.7 0.6 dynamic_slice.16
  1236.3 12.0 bitcast_add_fusion.2
  1248.3 20.1 %fusion.31 = f32[1,256,32,256]{3,1,2,0:T(8,128)S(1)} fusion(f32[1,256,32,256]{3,2,1,0:T(8,128)} %get-tuple-element.53, f32[1,256,32,256]{3,1,2,0:T(8,128)} %collective-permute-done, f32[3,256,32,256]{3,1,2,0:T(8,128)} %convolution_bitcast_fusion, pred[]{:T(512)S(6)} %eq.10), kind=kOutput, calls=%fused_computation.41 | convolution fusion | flops 6447693824 | bytes 33554432 | tf_op jit(solution)/shard_map/pkxy,kz->pzxy/dot_general | solution.py:57
  1268.4 8.3 copy.23
  1276.7 0.0 all-to-all-done.2
  1276.7 5.3 all-to-all-start.1
  1281.9 4.3 copy.28
  1286.2 9.7 fusion.50
  1295.9 21.5 %fusion.40 = f32[1,32,256,256]{3,2,1,0:T(8,128)} fusion(f32[256,32,256]{2,0,1:T(8,128)S(1)} %fusion.50), kind=kOutput, calls=%fused_computation.44 | convolution fusion | flops 6443499520 | bytes 16777216 | tf_op jit(solution)/shard_map/pzxk,ky->pzxy/dot_general | solution.py:63
  1317.5 148.3 %all-to-all-done.1 = f32[1,256,32,256]{3,2,0,1:T(8,128)} async-done(((f32[1,256,32,256]{3,2,0,1:T(8,128)}), f32[1,256,32,256]{3,2,0,1:T(8,128)}, u32[]{:S(2)}, u32[]{:S(2)}) %all-to-all-start.1) | async-done | bytes 8388640 | tf_op jit(solution)/shard_map/all_to_all | solution.py:112
  1465.8 4.3 copy.24
  1470.1 9.7 fusion.55
  1479.8 11.2 fusion.37
  (2 shorter events, 0.0 us)
Async XLA Ops:
  92.4 549.8 %all-to-all-start = ((f32[3,32,256,256]{3,1,0,2:T(8,128)}), f32[3,32,256,256]{3,1,0,2:T(8,128)}, u32[]{:S(2)}, u32[]{:S(2)}) async-start(f32[3,32,256,256]{3,1,0,2:T(8,128)} %copy.16), calls=%async_computation | async-start | bytes 50331648 | tf_op jit(solution)/shard_map/all_to_all | solution.py:68
  98.8 1107.2 %all-gather.3.cloned.1.call-start = ((), (), s32[]{:S(2)}) async-start(), calls=%async_computation.3 | async-start | bytes 41943040 | tf_op jit(solution)/shard_map/all_gather | solution.py:22
  704.5 184.1 %collective-permute-start = (f32[1,256,32,256]{3,1,2,0:T(8,128)}, f32[1,256,32,256]{3,1,2,0:T(8,128)}, u32[]{:S(2)}, u32[]{:S(2)}) collective-permute-start(f32[1,256,32,256]{3,1,2,0:T(8,128)} %fusion.22), channel_id=1, source_target_pairs={{0,8},{8,16},{16,24},{1,9},{9,17},{17,25},{2,10},{10,18},{18,26},{... | collective-permute-start | bytes 25165832 | tf_op jit(solution)/shard_map/ppermute | solution.py:17
  898.6 3.4 copy-start
  933.6 5.1 copy-start.1
  933.6 343.1 %all-to-all-start.2 = ((f32[1,256,32,256]{3,2,0,1:T(8,128)}), f32[1,256,32,256]{3,2,0,1:T(8,128)}, u32[]{:S(2)}, u32[]{:S(2)}) async-start(f32[1,256,32,256]{3,2,0,1:T(8,128)} %copy.27), calls=%async_computation.2 | async-start | bytes 16777216 | tf_op jit(solution)/shard_map/all_to_all | solution.py:108
  1276.7 189.1 %all-to-all-start.1 = ((f32[1,256,32,256]{3,2,0,1:T(8,128)}), f32[1,256,32,256]{3,2,0,1:T(8,128)}, u32[]{:S(2)}, u32[]{:S(2)}) async-start(f32[1,256,32,256]{3,2,0,1:T(8,128)} %copy.23), calls=%async_computation.1 | async-start | bytes 16777216 | tf_op jit(solution)/shard_map/all_to_all | solution.py:112
Sparse Core Ops, SparseCore 0:
  910.4 295.6 all-gather.2
where the time goes:
time: 1500 us
  waiting for transfers between devices  1130 us (75%)
  matrix products  177 us (12%)
  local copies, waits for them, and re-layouts  89.1 us (6%)
  other arithmetic  59.2 us (4%)
  starting transfers between devices  18 us (1%)
  between operations  15.1 us (1%)
    all_to_all x1, waiting for transfers between devices, on_device(): lax.all_to_all(planar_forward(stacked, hartley), 'space', split_axis=2, c...  542 us
    all_gather x1, waiting for transfers between devices, prefix(): gathered = jax.tree.map(lambda a: lax.all_gather(a, axis), part)  257 us
    ppermute x1, waiting for transfers between devices, shifted(): return lax.ppermute(array, axis, pairs)  183 us
    all_to_all x1, waiting for transfers between devices, on_device(): lax.all_to_all(depth_inverse(updated), 'space', split_axis=1, concat_axis...  148 us
    add x3, other arithmetic, compose(): jnp.exp(latter[0] * coarse_log) * former[1] + latter[1]  36 us
    dot_general x2, matrix products, depth_inverse(): return jnp.einsum('pkxy,kz->pzxy', spectrum, hartley, precision=highest)  33.2 us
    dot_general x1, matrix products, planar_forward(): return jnp.einsum('pzxy,kx->pzky', rows_done, hartley, precision=highest)  33 us
    dot_general x2, matrix products, planar_tail(): return jnp.einsum('pzxk,ky->pzxy', blocks, hartley, precision=highest)  32.8 us
  transfers between devices with their start and end apart: 5, of which 4 were waited for; matrix products, arithmetic and copies ran while one was open for 9% of the time, Pallas kernels for 0%

commit v1 on v0

v1 whole, which is shorter than its diff:
```python
import math

import jax
import jax.numpy as jnp
from jax import lax
from jax.sharding import PartitionSpec as P

FINE = 8
CHUNKS = 4


def einsum(spec, *operands):
    return jnp.einsum(spec, *operands, precision=lax.Precision.HIGH)


def hartley_table(extent):
    wavenumber = jnp.arange(extent, dtype=jnp.int32)
    product = wavenumber[:, None] * wavenumber[None, :] % extent
    angles = product.astype(jnp.float32) * (2.0 * math.pi / extent)
    return (jnp.cos(angles) + jnp.sin(angles)) * (1.0 / math.sqrt(extent))


def lattice_symbol(wavenumber, extent):
    angles = (wavenumber % extent).astype(jnp.float32) * (2.0 * math.pi / extent)
    return 2.0 - 2.0 * jnp.cos(angles)


def on_device(states, forcing, inflow, timestep):
    planes, extent = states.shape[1], states.shape[2]
    owners = lax.axis_size("space")
    intervals = lax.axis_size("tm")
    place = lax.axis_index("tm")
    rows = planes // CHUNKS
    share = planes // intervals
    hartley = hartley_table(extent)
    stepsize = timestep[0]
    owned = hartley.reshape(owners, planes, extent)

    def swap(blocks):
        return lax.all_to_all(blocks, "space", split_axis=0, concat_axis=0, tiled=True)

    def forward(rows_done, table, after=()):
        blocks = einsum("pzxc,okx->ozpkc", rows_done, table)
        blocks, _ = lax.optimization_barrier((blocks, after))
        sent = swap(blocks)
        return einsum("zpkc,lz->plkc", sent.reshape((extent,) + sent.shape[2:]), hartley)

    rows_states = einsum("pzxy,cy->pzxc", jnp.concatenate([states, forcing], axis=0), hartley)
    rows_inflow = einsum("zxy,cy->zxc", inflow, hartley)[None]

    mine = lax.dynamic_slice_in_dim(owned, place * share, share, 1)
    spec_inflow = lax.all_gather(forward(rows_inflow, mine)[0], "tm")
    spec_inflow = jnp.moveaxis(spec_inflow, 0, 1).reshape(extent, planes, extent)

    full_symbol = lattice_symbol(jnp.arange(extent, dtype=jnp.int32), extent)
    shift_pairs = [(i, i + 1) for i in range(intervals - 1)]
    first = lax.axis_index("space") * planes
    states_back, defects_back, defects, advances, arrivals = [], [], [], [], []
    for chunk in range(CHUNKS):
        lo = chunk * rows
        after = (advances[chunk - 2 : chunk - 1] if chunk >= 2 else [], arrivals[: max(chunk - 2, 0)])
        spectra = forward(rows_states, owned[:, lo : lo + rows], after)
        column = first + lo + jnp.arange(rows, dtype=jnp.int32)
        laplace = (
            full_symbol[:, None, None]
            + lattice_symbol(column, extent)[None, :, None]
            + full_symbol[None, None, :]
        )
        damping = 1.0 / (1.0 + stepsize * laplace)
        coarse = 1.0 / (1.0 + FINE * stepsize * laplace)
        propagator = jnp.ones_like(damping)
        accrued = jnp.zeros_like(damping)
        for repeat in range(FINE):
            propagator = propagator * damping
            accrued = accrued + propagator
        advanced = propagator * spectra[0] + stepsize * accrued * spectra[1]
        advanced, _ = lax.optimization_barrier((advanced, defects[: max(chunk - 1, 0)]))
        arrived = lax.ppermute(advanced, "tm", shift_pairs)
        advances.append(advanced)
        arrivals.append(arrived)
        relaxed = jnp.where(place == 0, spec_inflow[:, lo : lo + rows], arrived)
        defect = propagator * (relaxed - spectra[0])
        defects.append(defect)

        def backward(spectrum):
            got = swap(einsum("lkc,lz->zkc", spectrum, hartley).reshape(owners, planes, rows, extent))
            return einsum("ozkc,cy->zoky", got, hartley)

        defects_back.append(backward(defect))
        gathered = lax.all_gather(defect, "tm")
        correction = jnp.zeros_like(defect)
        for i in range(intervals - 1):
            correction = jnp.where(i < place, coarse * correction + gathered[i], correction)
        states_back.append(backward(relaxed + correction))

    def width_inverse(pieces):
        blocks = jnp.concatenate(pieces, axis=2).reshape(planes, extent, extent)
        return einsum("zky,kx->zxy", blocks, hartley)[None]

    return width_inverse(states_back), width_inverse(defects_back)


def solution(mesh):
    return jax.shard_map(
        on_device,
        mesh=mesh,
        in_specs=(
            P("tm", "space", None, None),
            P("tm", "space", None, None),
            P("space", None, None),
            P(),
        ),
        out_specs=(P("tm", "space", None, None), P("tm", "space", None, None)),
        check_vma=False,
    )
```

time: 1500 us -> 1100 us (0.73)
  waiting for transfers between devices: 1130 us -> 728 us
  local copies, waits for them, and re-layouts: 89.1 us -> 38.1 us
  starting transfers between devices: 18 us -> 65.8 us
  matrix products: 177 us -> 217 us
  other arithmetic: 59.2 us -> 24 us
    all_gather x1 -> x5, waiting for transfers between devices: 257 us -> 0.08 us  [the longest x4 0.08 us: on_device(): gathered = lax.all_gather(defect, 'tm')]
    all_to_all x3 -> x13, waiting for transfers between devices: 691 us -> 594 us  [swap(): lax.all_to_all(blocks, 'space', split_axis=0, concat_axis=0, tiled=True)]
    ppermute x1 -> x4, waiting for transfers between devices: 183 us -> 133 us  [on_device(): arrived = lax.ppermute(advanced, 'tm', shift_pairs)]
    all_to_all x3 -> x13, starting transfers between devices: 16.7 us -> 60.3 us  [swap(): lax.all_to_all(blocks, 'space', split_axis=0, concat_axis=0, tiled=True)]
    dot_general x9 -> x30, matrix products: 177 us -> 217 us  [einsum(): return jnp.einsum(spec, *operands, precision=lax.Precision.HIGH)]
    transpose x3 -> x1, local copies, waits for them, and re-layouts: 43.5 us -> 4.11 us  [on_device(): jnp.moveaxis(spec_inflow, 0, 1).reshape(extent, planes, extent)]
    add x5 -> x3, other arithmetic: 48.1 us -> 10.1 us  [the longest x2 10.1 us: on_device(): advanced = propagator * spectra[0] + stepsize * accrued * spectra[1]]
  transfers between devices with their start and end apart: 5 -> 22, of which waited for: 4 -> 14; matrix products, arithmetic and copies ran while one was open for 9% -> 20% of each run, Pallas kernels for 0% -> 0%
where the time goes in v1:
time: 1100 us; the launch traced here: 1090 us
  waiting for transfers between devices  728 us (66%)
  matrix products  217 us (20%)
  starting transfers between devices  65.8 us (6%)
  local copies, waits for them, and re-layouts  38.1 us (3%)
  other arithmetic  24 us (2%)
  between operations  15.4 us (1%)
    all_to_all x13, waiting for transfers between devices, swap(): lax.all_to_all(blocks, 'space', split_axis=0, concat_axis=0, tiled=True)  594 us
    dot_general x30, matrix products, einsum(): return jnp.einsum(spec, *operands, precision=lax.Precision.HIGH)  217 us
    ppermute x4, waiting for transfers between devices, on_device(): arrived = lax.ppermute(advanced, 'tm', shift_pairs)  133 us
    all_to_all x13, starting transfers between devices, swap(): lax.all_to_all(blocks, 'space', split_axis=0, concat_axis=0, tiled=True)  60.3 us
  transfers between devices with their start and end apart: 22, of which 14 were waited for; matrix products, arithmetic and copies ran while one was open for 20% of the time, Pallas kernels for 0%

profile of v1, /device:TPU:6, one launch (start us, length us, event | category | flops | bytes accessed | tf_op | source)
XLA Modules:
  0.0 1088.4 jit_solution(3783311885844711203)
XLA Ops:
  8.3 15.5 %fusion.230 = f32[256,32,256]{2,0,1:T(8,128)} fusion(f32[32,256,256]{2,1,0:T(8,128)} %param.6), kind=kOutput, calls=%fused_computation.252 | convolution fusion | flops 3222274048 | bytes 16777216 | tf_op jit(solution)/shard_map/zxy,cy->zxc/dot_general | solution.py:13
  23.8 8.6 fusion.176
  32.4 5.1 all-to-all-start
  37.5 15.8 %fusion = f32[2,32,256,256]{3,2,1,0:T(8,128)} fusion(f32[1,32,256,256]{3,2,1,0:T(8,128)} %param.5, f32[1,32,256,256]{3,2,1,0:T(8,128)} %param.4), kind=kOutput, calls=%fused_computation | convolution fusion | flops 6447693824 | bytes 33554432 | tf_op jit(solution)/shard_map/pzxy,cy->pzxc/dot_general | solution.py:13
  53.3 13.8 %fusion.84 = f32[8,32,2,8,256]{4,3,1,2,0:T(8,128)} fusion(f32[2,32,256,256]{3,2,1,0:T(8,128)} %fusion, f32[8,32,256]{2,1,0:T(8,128)S(1)} %add_multiply_fusion.8), kind=kOutput, calls=%fused_computation.90 | convolution fusion | flops 1610612736 | bytes 21037056 | tf_op jit(solution)/shard_map/pzxc,okx->ozpkc/dot_general | solution.py:13
  67.1 19.4 %all-to-all-done = f32[8,32,1,8,256]{4,3,1,2,0:T(8,128)S(1)} async-done(((f32[8,32,1,8,256]{4,3,1,2,0:T(8,128)}), f32[8,32,1,8,256]{4,3,1,2,0:T(8,128)S(1)}, u32[]{:S(2)}, u32[]{:S(2)}) %all-to-all-start) | async-done | bytes 2097184 | tf_op jit(solution)/shard_map/all_to_all | solution.py:40
  86.5 5.0 all-to-all-start.1
  91.5 13.8 %fusion.87 = f32[8,32,2,8,256]{4,3,1,2,0:T(8,128)} fusion(f32[2,32,256,256]{3,2,1,0:T(8,128)} %fusion, f32[8,32,256]{2,1,0:T(8,128)S(1)} %add_multiply_fusion.8), kind=kOutput, calls=%fused_computation.91 | convolution fusion | flops 1610612736 | bytes 21037056 | tf_op jit(solution)/shard_map/pzxc,okx->ozpkc/dot_general | solution.py:13
  105.3 80.2 %all-to-all-done.1 = f32[8,32,2,8,256]{4,3,1,2,0:T(8,128)} async-done(((f32[8,32,2,8,256]{4,3,1,2,0:T(8,128)}), f32[8,32,2,8,256]{4,3,1,2,0:T(8,128)}, u32[]{:S(2)}, u32[]{:S(2)}) %all-to-all-start.1) | async-done | bytes 4194336 | tf_op jit(solution)/shard_map/all_to_all | solution.py:40
  185.5 4.5 all-to-all-start.3
  195.6 13.8 %fusion.90 = f32[8,32,2,8,256]{4,3,1,2,0:T(8,128)} fusion(f32[2,32,256,256]{3,2,1,0:T(8,128)} %fusion, f32[8,32,256]{2,1,0:T(8,128)S(1)} %add_multiply_fusion.8), kind=kOutput, calls=%fused_computation.92 | convolution fusion | flops 1610612736 | bytes 21037056 | tf_op jit(solution)/shard_map/pzxc,okx->ozpkc/dot_general | solution.py:13
  212.1 5.1 fusion.72
  222.0 62.0 %all-to-all-done.3 = f32[8,32,2,8,256]{4,3,1,2,0:T(8,128)} async-done(((f32[8,32,2,8,256]{4,3,1,2,0:T(8,128)}), f32[8,32,2,8,256]{4,3,1,2,0:T(8,128)}, u32[]{:S(2)}, u32[]{:S(2)}) %all-to-all-start.3) | async-done | bytes 4194336 | tf_op jit(solution)/shard_map/all_to_all | solution.py:40
  284.0 4.8 all-to-all-start.5
  292.9 7.1 fusion.75
  300.0 82.6 %all-to-all-done.5 = f32[8,32,2,8,256]{4,3,1,2,0:T(8,128)} async-done(((f32[8,32,2,8,256]{4,3,1,2,0:T(8,128)}), f32[8,32,2,8,256]{4,3,1,2,0:T(8,128)}, u32[]{:S(2)}, u32[]{:S(2)}) %all-to-all-start.5) | async-done | bytes 4194336 | tf_op jit(solution)/shard_map/all_to_all | solution.py:40
  385.3 6.9 fusion.78
  402.3 7.4 fusion.103
  409.8 13.8 %fusion.93 = f32[8,32,2,8,256]{4,3,1,2,0:T(8,128)} fusion(f32[2,32,256,256]{3,2,1,0:T(8,128)} %fusion, f32[8,32,256]{2,1,0:T(8,128)S(1)} %add_multiply_fusion.8), kind=kOutput, calls=%fused_computation.93 | convolution fusion | flops 1610612736 | bytes 21037056 | tf_op jit(solution)/shard_map/pzxc,okx->ozpkc/dot_general | solution.py:13
  423.6 4.6 all-to-all-start.7
  431.0 91.2 %all-to-all-done.7 = f32[8,32,2,8,256]{4,3,1,2,0:T(8,128)} async-done(((f32[8,32,2,8,256]{4,3,1,2,0:T(8,128)}), f32[8,32,2,8,256]{4,3,1,2,0:T(8,128)}, u32[]{:S(2)}, u32[]{:S(2)}) %all-to-all-start.7) | async-done | bytes 4194336 | tf_op jit(solution)/shard_map/all_to_all | solution.py:40
  525.1 5.1 fusion.81
  530.2 46.6 %collective-permute-done.1 = f32[256,8,256]{2,0,1:T(8,128)S(1)} collective-permute-done((f32[256,8,256]{2,0,1:T(8,128)}, f32[256,8,256]{2,0,1:T(8,128)S(1)}, u32[]{:S(2)}, u32[]{:S(2)}) %collective-permute-start.1) | collective-permute-done | bytes 2097184 | tf_op jit(solution)/shard_map/ppermute | solution.py:78
  576.9 7.2 subtract_multiply_fusion.1
  589.2 4.7 all-to-all-start.9
  597.5 45.5 %all-to-all-done.9 = f32[8,32,8,256]{3,1,2,0:T(8,128)} async-done(((f32[8,32,8,256]{3,1,2,0:T(8,128)}), f32[8,32,8,256]{3,1,2,0:T(8,128)}, u32[]{:S(2)}, u32[]{:S(2)}) %all-to-all-start.9) | async-done | bytes 2097184 | tf_op jit(solution)/shard_map/all_to_all | solution.py:40
  643.1 4.6 all-to-all-start.11
  651.3 45.3 %all-to-all-done.11 = f32[8,32,8,256]{3,1,2,0:T(8,128)} async-done(((f32[8,32,8,256]{3,1,2,0:T(8,128)}), f32[8,32,8,256]{3,1,2,0:T(8,128)}, u32[]{:S(2)}, u32[]{:S(2)}) %all-to-all-start.11) | async-done | bytes 2097184 | tf_op jit(solution)/shard_map/all_to_all | solution.py:40
  696.7 4.4 all-to-all-start.10
  702.4 86.1 %collective-permute-done.3 = f32[256,8,256]{2,0,1:T(8,128)S(1)} collective-permute-done((f32[256,8,256]{2,0,1:T(8,128)S(1)}, f32[256,8,256]{2,0,1:T(8,128)S(1)}, u32[]{:S(2)}, u32[]{:S(2)}) %collective-permute-start.3) | collective-permute-done | bytes 2097184 | tf_op jit(solution)/shard_map/ppermute | solution.py:78
  796.2 4.7 all-to-all-start.12
  801.5 7.2 fusion.148
  810.2 39.7 %all-to-all-done.12 = f32[8,32,8,256]{3,1,2,0:T(8,128)S(1)} async-done(((f32[8,32,8,256]{3,1,2,0:T(8,128)}), f32[8,32,8,256]{3,1,2,0:T(8,128)S(1)}, u32[]{:S(2)}, u32[]{:S(2)}) %all-to-all-start.12) | async-done | bytes 2097184 | tf_op jit(solution)/shard_map/all_to_all | solution.py:40
  849.9 4.8 all-to-all-start.2
  854.7 7.2 fusion.136
  863.4 40.3 %all-to-all-done.2 = f32[8,32,8,256]{3,1,2,0:T(8,128)} async-done(((f32[8,32,8,256]{3,1,2,0:T(8,128)}), f32[8,32,8,256]{3,1,2,0:T(8,128)}, u32[]{:S(2)}, u32[]{:S(2)}) %all-to-all-start.2) | async-done | bytes 2097184 | tf_op jit(solution)/shard_map/all_to_all | solution.py:40
  903.7 4.4 all-to-all-start.6
  908.1 7.2 fusion.142
  916.8 40.4 %all-to-all-done.6 = f32[8,32,8,256]{3,1,2,0:T(8,128)} async-done(((f32[8,32,8,256]{3,1,2,0:T(8,128)}), f32[8,32,8,256]{3,1,2,0:T(8,128)}, u32[]{:S(2)}, u32[]{:S(2)}) %all-to-all-start.6) | async-done | bytes 2097184 | tf_op jit(solution)/shard_map/all_to_all | solution.py:40
  957.1 4.4 all-to-all-start.4
  961.5 7.2 fusion.130
  970.2 40.4 %all-to-all-done.4 = f32[8,32,8,256]{3,1,2,0:T(8,128)} async-done(((f32[8,32,8,256]{3,1,2,0:T(8,128)}), f32[8,32,8,256]{3,1,2,0:T(8,128)}, u32[]{:S(2)}, u32[]{:S(2)}) %all-to-all-start.4) | async-done | bytes 2097184 | tf_op jit(solution)/shard_map/all_to_all | solution.py:40
  1010.5 4.5 all-to-all-start.8
  1029.5 12.3 %fusion.29 = f32[1,32,256,256]{3,2,1,0:T(8,128)} fusion(f32[32,256,256]{2,0,1:T(8,128)S(1)} %bitcast.248), kind=kOutput, calls=%fused_computation.37 | convolution fusion | flops 3222274048 | bytes 16777216 | tf_op jit(solution)/shard_map/zky,kx->zxy/dot_general | solution.py:13
  1045.5 5.9 convolution_bitcast_fusion.5
  1051.4 5.6 convolution_bitcast_fusion.6
  1057.0 7.1 all-to-all-done.8
  1069.1 12.3 %fusion.26 = f32[1,32,256,256]{3,2,1,0:T(8,128)} fusion(f32[32,256,256]{2,0,1:T(8,128)S(1)} %bitcast.249), kind=kOutput, calls=%fused_computation.36 | convolution fusion | flops 3222274048 | bytes 16777216 | tf_op jit(solution)/shard_map/zky,kx->zxy/dot_general | solution.py:13
  (96 shorter events, 87.1 us)
Async XLA Ops:
  32.4 54.1 %all-to-all-start = ((f32[8,32,1,8,256]{4,3,1,2,0:T(8,128)}), f32[8,32,1,8,256]{4,3,1,2,0:T(8,128)S(1)}, u32[]{:S(2)}, u32[]{:S(2)}) async-start(f32[8,32,1,8,256]{4,3,1,2,0:T(8,128)} %bitcast.260), calls=%async_computation | async-start | bytes 4194304 | tf_op jit(solution)/shard_map/all_to_all | solution.py:40
  86.5 98.9 %all-to-all-start.1 = ((f32[8,32,2,8,256]{4,3,1,2,0:T(8,128)}), f32[8,32,2,8,256]{4,3,1,2,0:T(8,128)}, u32[]{:S(2)}, u32[]{:S(2)}) async-start(f32[8,32,2,8,256]{4,3,1,2,0:T(8,128)} %fusion.84), calls=%async_computation.1 | async-start | bytes 8388608 | tf_op jit(solution)/shard_map/all_to_all | solution.py:40
  185.5 98.5 %all-to-all-start.3 = ((f32[8,32,2,8,256]{4,3,1,2,0:T(8,128)}), f32[8,32,2,8,256]{4,3,1,2,0:T(8,128)}, u32[]{:S(2)}, u32[]{:S(2)}) async-start(f32[8,32,2,8,256]{4,3,1,2,0:T(8,128)} %fusion.87), calls=%async_computation.3 | async-start | bytes 8388608 | tf_op jit(solution)/shard_map/all_to_all | solution.py:40
  190.0 202.2 %all-gather.11.cloned.1.call-start = ((), (), s32[]{:S(2)}) async-start(), calls=%async_computation.13 | async-start | bytes 10485760 | tf_op jit(solution)/shard_map/all_gather | solution.py:52
  217.3 2.1 copy-start.2
  284.0 98.5 %all-to-all-start.5 = ((f32[8,32,2,8,256]{4,3,1,2,0:T(8,128)}), f32[8,32,2,8,256]{4,3,1,2,0:T(8,128)}, u32[]{:S(2)}, u32[]{:S(2)}) async-start(f32[8,32,2,8,256]{4,3,1,2,0:T(8,128)} %fusion.90), calls=%async_computation.5 | async-start | bytes 8388608 | tf_op jit(solution)/shard_map/all_to_all | solution.py:40
  288.8 512.8 %all-gather.13.cloned.1.call-start = ((), (), s32[]{:S(2)}) async-start(), calls=%async_computation.14 | async-start | bytes 10485760 | tf_op jit(solution)/shard_map/all_gather | solution.py:90
  288.8 107.6 %collective-permute-start = (f32[256,8,256]{2,0,1:T(8,128)}, f32[256,8,256]{2,0,1:T(8,128)}, u32[]{:S(2)}, u32[]{:S(2)}) collective-permute-start(f32[256,8,256]{2,0,1:T(8,128)} %fusion.111), channel_id=1, source_target_pairs={{0,8},{8,16},{16,24},{1,9},{9,17},{17,25},{2,10},{10,18},{18,26},{... | collective-permute-start | bytes 6291464 | tf_op jit(solution)/shard_map/ppermute | solution.py:78
  392.2 4.6 copy-start.3
  392.2 7.6 copy-start.4
  392.2 10.1 copy-start.6
  396.4 13.4 %copy-start = (f32[256,4,8,256]{3,0,2,1:T(8,128)}, f32[256,4,8,256]{3,0,2,1:T(8,128)S(1)}, u32[]{:S(2)}) copy-start(f32[256,4,8,256]{3,0,2,1:T(8,128)S(1)} %copy.71) | copy-start | bytes 25165828
  423.6 98.5 %all-to-all-start.7 = ((f32[8,32,2,8,256]{4,3,1,2,0:T(8,128)}), f32[8,32,2,8,256]{4,3,1,2,0:T(8,128)}, u32[]{:S(2)}, u32[]{:S(2)}) async-start(f32[8,32,2,8,256]{4,3,1,2,0:T(8,128)} %fusion.93), calls=%async_computation.7 | async-start | bytes 8388608 | tf_op jit(solution)/shard_map/all_to_all | solution.py:40
  428.2 426.6 %all-gather.17.cloned.1.call-start = ((), (), s32[]{:S(2)}) async-start(), calls=%async_computation.16 | async-start | bytes 10485760 | tf_op jit(solution)/shard_map/all_gather | solution.py:90
  428.2 102.0 %collective-permute-start.2 = (f32[256,8,256]{2,0,1:T(8,128)}, f32[256,8,256]{2,0,1:T(8,128)}, u32[]{:S(2)}, u32[]{:S(2)}) collective-permute-start(f32[256,8,256]{2,0,1:T(8,128)} %get-tuple-element.7), channel_id=1, source_target_pairs={{0,8},{8,16},{16,24},{1,9},{9,17},{17,25},{2,10},{10,18},{18,26},{... | collective-permute-start | bytes 6291464 | tf_op jit(solution)/shard_map/ppermute | solution.py:78
  429.5 147.3 %collective-permute-start.1 = (f32[256,8,256]{2,0,1:T(8,128)}, f32[256,8,256]{2,0,1:T(8,128)S(1)}, u32[]{:S(2)}, u32[]{:S(2)}) collective-permute-start(f32[256,8,256]{2,0,1:T(8,128)} %get-tuple-element.14), channel_id=1, source_target_pairs={{0,8},{8,16},{16,24},{1,9},{9,17},{17,25},{2,10},{10,18},{18,26},{... | collective-permute-start | bytes 6291464 | tf_op jit(solution)/shard_map/ppermute | solution.py:78
  522.1 54.7 %slice-start = ((s8[8388608]{0:T(1024)(128)(4,1)}), s8[4194304]{0:T(1024)(128)(4,1)S(1)}, s32[]{:S(2)}) async-start(s8[8388608]{0:T(1024)(128)(4,1)} %bitcast.245), calls=%async_computation.18 | async-start | bytes 8388608
  522.1 54.7 %copy-start.7 = (f32[2,256,8,256]{3,1,2,0:T(8,128)S(1)}, f32[2,256,8,256]{3,1,2,0:T(8,128)}, u32[]{:S(2)}) copy-start(f32[2,256,8,256]{3,1,2,0:T(8,128)} %fusion.78) | copy-start | bytes 12582916
  525.1 51.8 %slice-start.1 = ((s8[8388608]{0:T(1024)(128)(4,1)}), s8[4194304]{0:T(1024)(128)(4,1)S(1)}, s32[]{:S(2)}) async-start(s8[8388608]{0:T(1024)(128)(4,1)} %bitcast.245), calls=%async_computation.19 | async-start | bytes 8388608
  525.1 51.8 %copy-start.5 = (f32[2,256,8,256]{3,1,2,0:T(8,128)S(1)}, f32[2,256,8,256]{3,1,2,0:T(8,128)}, u32[]{:S(2)}) copy-start(f32[2,256,8,256]{3,1,2,0:T(8,128)} %fusion.75) | copy-start | bytes 12582916
  530.2 53.8 %copy-start.1 = (f32[2,256,8,256]{3,1,2,0:T(8,128)}, f32[2,256,8,256]{3,1,2,0:T(8,128)S(1)}, u32[]{:S(2)}) copy-start(f32[2,256,8,256]{3,1,2,0:T(8,128)S(1)} %fusion.81) | copy-start | bytes 12582916
  576.8 7.2 copy-start.14
  584.0 1.6 copy-start.8
  584.1 324.1 %all-gather.15.cloned.1.call-start = ((), (), s32[]{:S(2)}) async-start(), calls=%async_computation.15 | async-start | bytes 10485760 | tf_op jit(solution)/shard_map/all_gather | solution.py:90
  589.2 4.7 copy-start.10
  589.2 53.9 %all-to-all-start.9 = ((f32[8,32,8,256]{3,1,2,0:T(8,128)}), f32[8,32,8,256]{3,1,2,0:T(8,128)}, u32[]{:S(2)}, u32[]{:S(2)}) async-start(f32[8,32,8,256]{3,1,2,0:T(8,128)} %copy.94), calls=%async_computation.9 | async-start | bytes 4194304 | tf_op jit(solution)/shard_map/all_to_all | solution.py:40
  597.5 50.1 %copy-start.9 = (f32[256,8,256]{2,0,1:T(8,128)S(1)}, f32[256,8,256]{2,0,1:T(8,128)}, u32[]{:S(2)}) copy-start(f32[256,8,256]{2,0,1:T(8,128)} %get-tuple-element.11) | copy-start | bytes 6291460
  643.1 53.6 %all-to-all-start.11 = ((f32[8,32,8,256]{3,1,2,0:T(8,128)}), f32[8,32,8,256]{3,1,2,0:T(8,128)}, u32[]{:S(2)}, u32[]{:S(2)}) async-start(f32[8,32,8,256]{3,1,2,0:T(8,128)} %copy.98), calls=%async_computation.11 | async-start | bytes 4194304 | tf_op jit(solution)/shard_map/all_to_all | solution.py:40
  651.3 49.7 %copy-start.15 = (f32[256,8,256]{2,0,1:T(8,128)S(1)}, f32[256,8,256]{2,0,1:T(8,128)}, u32[]{:S(2)}) copy-start(f32[256,8,256]{2,0,1:T(8,128)} %get-tuple-element.9) | copy-start | bytes 6291460
  696.7 99.5 %all-to-all-start.10 = ((f32[8,32,8,256]{3,1,2,0:T(8,128)}), f32[8,32,8,256]{3,1,2,0:T(8,128)}, u32[]{:S(2)}, u32[]{:S(2)}) async-start(f32[8,32,8,256]{3,1,2,0:T(8,128)} %copy.96), calls=%async_computation.10 | async-start | bytes 4194304 | tf_op jit(solution)/shard_map/all_to_all | solution.py:40
  701.1 87.4 %collective-permute-start.3 = (f32[256,8,256]{2,0,1:T(8,128)S(1)}, f32[256,8,256]{2,0,1:T(8,128)S(1)}, u32[]{:S(2)}, u32[]{:S(2)}) collective-permute-start(f32[256,8,256]{2,0,1:T(8,128)S(1)} %copy-done.15), channel_id=1, source_target_pairs={{0,8},{8,16},{16,24},{1,9},{9,17},{17,25},{2,10},{10,18},{18,26},{... | collective-permute-start | bytes 6291464 | tf_op jit(solution)/shard_map/ppermute | solution.py:78
  788.5 1.3 copy-start.16
  792.6 2.1 copy-start.11
  796.2 53.7 %all-to-all-start.12 = ((f32[8,32,8,256]{3,1,2,0:T(8,128)}), f32[8,32,8,256]{3,1,2,0:T(8,128)S(1)}, u32[]{:S(2)}, u32[]{:S(2)}) async-start(f32[8,32,8,256]{3,1,2,0:T(8,128)} %copy.100), calls=%async_computation.12 | async-start | bytes 4194304 | tf_op jit(solution)/shard_map/all_to_all | solution.py:40
  800.9 160.6 %all-gather.19.cloned.1.call-start = ((), (), s32[]{:S(2)}) async-start(), calls=%async_computation.17 | async-start | bytes 10485760 | tf_op jit(solution)/shard_map/all_gather | solution.py:90
  849.9 53.8 %all-to-all-start.2 = ((f32[8,32,8,256]{3,1,2,0:T(8,128)}), f32[8,32,8,256]{3,1,2,0:T(8,128)}, u32[]{:S(2)}, u32[]{:S(2)}) async-start(f32[8,32,8,256]{3,1,2,0:T(8,128)} %copy.76), calls=%async_computation.2 | async-start | bytes 4194304 | tf_op jit(solution)/shard_map/all_to_all | solution.py:40
  903.7 53.4 %all-to-all-start.6 = ((f32[8,32,8,256]{3,1,2,0:T(8,128)}), f32[8,32,8,256]{3,1,2,0:T(8,128)}, u32[]{:S(2)}, u32[]{:S(2)}) async-start(f32[8,32,8,256]{3,1,2,0:T(8,128)} %copy.86), calls=%async_computation.6 | async-start | bytes 4194304 | tf_op jit(solution)/shard_map/all_to_all | solution.py:40
  957.1 53.4 %all-to-all-start.4 = ((f32[8,32,8,256]{3,1,2,0:T(8,128)}), f32[8,32,8,256]{3,1,2,0:T(8,128)}, u32[]{:S(2)}, u32[]{:S(2)}) async-start(f32[8,32,8,256]{3,1,2,0:T(8,128)} %copy.81), calls=%async_computation.4 | async-start | bytes 4194304 | tf_op jit(solution)/shard_map/all_to_all | solution.py:40
  1010.5 53.6 %all-to-all-start.8 = ((f32[8,32,8,256]{3,1,2,0:T(8,128)}), f32[8,32,8,256]{3,1,2,0:T(8,128)}, u32[]{:S(2)}, u32[]{:S(2)}) async-start(f32[8,32,8,256]{3,1,2,0:T(8,128)} %copy.91), calls=%async_computation.8 | async-start | bytes 4194304 | tf_op jit(solution)/shard_map/all_to_all | solution.py:40
  1064.1 3.8 copy-start.12
  1064.1 3.8 copy-start.13
Sparse Core Ops, SparseCore 0:
  194.8 87.7 all-gather.10
  409.9 138.5 all-gather.12
  584.2 87.4 all-gather.16
  673.4 124.3 all-gather.14
  803.8 88.0 all-gather.18
